TPU v7x, 32 devices: a whole 2x2x4 slice. The times are simulated.
32 devices in a mesh: trans: 16 (over z, y, x), los: 2 (over core).
Axes of the slice: x: 2, y: 2, z: 4, core: 2. Of those that a mesh axis runs over, the one named last changes fastest.
Arguments:
- density: bfloat16 [2, 2048, 2048], P('los', 'trans'), may hold values from -6 to 6
- row_pos: float32 [2, 2048], replicated, may hold values from 0 to 2048
- col_pos: float32 [2, 2048], replicated, may hold values from 0 to 2048
- plane_of_slot: int32 [2], replicated, may hold values from 0 to 1, each once
- plane_bin: int32 [2], replicated, may hold values from 0 to 3, as said below
- efficiency: float32 [4, 2], replicated, may hold values from 0.3 to 3
Outputs:
- shear: float32 [2, 4, 2048, 2048], P(None, None, ('trans', 'los'))
Inputs may be any that keep to these rules, and one draw needn't show every extreme that they name: `plane_bin`: some plane has bin 0 and some plane has bin 4 - 1.
All inputs are finite; a program needn't handle non-finite values.
Results may differ from a plain program's by a relative error of at most 0.006.
Values may be sent and summed in bfloat16 or wider, within the bound.
A program may use at most 64 MiB of HBM per device.

v0:
```python
import math
import jax
import jax.numpy as jnp
from jax import lax
from jax.sharding import PartitionSpec as P


def hat_block(positions, mesh_cells):
    cells = jnp.arange(mesh_cells, dtype=jnp.int32).astype(jnp.float32)
    offset = positions[:, None] - cells[None, :] + 0.5 * mesh_cells
    folded = jnp.mod(offset, 1.0 * mesh_cells) - 0.5 * mesh_cells
    return jnp.maximum(1.0 - jnp.abs(folded), 0.0).astype(jnp.bfloat16)


def trig_pair(rows_n, cols_n, modulus, sign_value):
    product_index = (
        jnp.arange(rows_n, dtype=jnp.int32)[:, None]
        * jnp.arange(cols_n, dtype=jnp.int32)[None, :]
        % modulus
    )
    angle = product_index.astype(jnp.float32) * (2.0 * math.pi / modulus)
    return (jnp.cos(angle), sign_value * jnp.sin(angle))


def fourier(real_part, imag_part, inverse):
    length = real_part.shape[-1]
    factor_one = 16
    second = length // factor_one
    sign_value = 1.0 if inverse else -1.0
    lead_shape = real_part.shape[:-1]
    highest = lax.Precision.HIGHEST
    cos_one, sin_one = trig_pair(factor_one, factor_one, factor_one, sign_value)
    real_grid = real_part.reshape(lead_shape + (factor_one, second))
    imag_grid = imag_part.reshape(lead_shape + (factor_one, second))

    def first_pass(table, values):
        return jnp.einsum("kn,...nm->...km", table, values, precision=highest)

    section_real = first_pass(cos_one, real_grid) - first_pass(sin_one, imag_grid)
    section_imag = first_pass(cos_one, imag_grid) + first_pass(sin_one, real_grid)
    cos_twid, sin_twid = trig_pair(factor_one, second, length, sign_value)
    turned_real = section_real * cos_twid - section_imag * sin_twid
    turned_imag = section_real * sin_twid + section_imag * cos_twid
    cos_two, sin_two = trig_pair(second, second, second, sign_value)

    def second_pass(values, table):
        return jnp.einsum("...km,mj->...kj", values, table, precision=highest)

    out_real = second_pass(turned_real, cos_two) - second_pass(turned_imag, sin_two)
    out_imag = second_pass(turned_real, sin_two) + second_pass(turned_imag, cos_two)
    out_real = jnp.swapaxes(out_real, -1, -2).reshape(lead_shape + (length,))
    out_imag = jnp.swapaxes(out_imag, -1, -2).reshape(lead_shape + (length,))
    scale = 1.0 / length if inverse else 1.0
    return (out_real * scale, out_imag * scale)


def wave_numbers(index_all, length):
    return jnp.where(index_all < length // 2, index_all, index_all - length).astype(jnp.float32)


def body(density, row_pos, col_pos, plane_of_slot, plane_bin, efficiency):
    count_trans = lax.axis_size("trans")
    count_los = lax.axis_size("los")
    per_device = density.shape[0]
    mesh_cells = density.shape[2]
    grid_cells = row_pos.shape[1]
    planes_total = row_pos.shape[0]
    bins_total = efficiency.shape[0]
    width_cols = grid_cells // (count_trans * count_los)
    block_rows = min(512, grid_cells)
    slots = jnp.arange(planes_total, dtype=jnp.int32)
    bin_index = jnp.arange(bins_total, dtype=jnp.int32)
    by_columns = lax.all_to_all(density, "trans", split_axis=2, concat_axis=1, tiled=True)
    local_slot = 0
    slot_now = lax.axis_index("los") * per_device + local_slot
    plane_id = jnp.sum(jnp.where(slots == slot_now, plane_of_slot, 0))
    chosen = slots == plane_id
    plane_eff = jnp.sum(jnp.where(chosen[None, :], efficiency, 0.0), axis=1)
    first_bin = jnp.sum(jnp.where(chosen, plane_bin, 0))
    weight_list = [plane_eff * (bin_index >= first_bin).astype(jnp.float32)]
    rows_here = jnp.sum(jnp.where(chosen[:, None], row_pos, 0.0), axis=0)
    cols_here = jnp.sum(jnp.where(chosen[:, None], col_pos, 0.0), axis=0)
    pieces = []
    for begin in range(0, grid_cells, block_rows):
        row_block = hat_block(rows_here[begin : begin + block_rows], mesh_cells)
        pieces.append(
            lax.dot_general(
                by_columns[local_slot],
                row_block,
                (((0,), (1,)), ((), ())),
                preferred_element_type=jnp.float32,
            )
        )
    resampled = [jnp.concatenate(pieces, axis=1).astype(jnp.bfloat16)]
    col_tables = [hat_block(cols_here, mesh_cells)]
    half_columns = jnp.stack(resampled)
    exchanged = lax.all_to_all(half_columns, "trans", split_axis=2, concat_axis=1, tiled=True)
    local_slot = 0
    rows_map = lax.dot_general(
        exchanged[local_slot],
        col_tables[local_slot],
        (((0,), (1,)), ((), ())),
        preferred_element_type=jnp.float32,
    )
    plane_term = weight_list[local_slot][None, :, None] * rows_map[:, None, :]
    term_real, term_imag = fourier(plane_term, jnp.zeros_like(plane_term), False)
    summed_real, summed_imag = (
        lax.psum_scatter(term_real, "los", scatter_dimension=2, tiled=True),
        lax.psum_scatter(term_imag, "los", scatter_dimension=2, tiled=True),
    )
    arrived = lax.all_to_all(
        jnp.stack([summed_real, summed_imag]), "trans", split_axis=3, concat_axis=1, tiled=True
    )
    columns_local = arrived.transpose(0, 2, 3, 1)
    col_index = (
        lax.axis_index("los") * (grid_cells // count_los)
        + lax.axis_index("trans") * width_cols
        + jnp.arange(width_cols, dtype=jnp.int32)
    )
    freq_real, freq_imag = fourier(columns_local[0], columns_local[1], False)
    wave_rows = wave_numbers(jnp.arange(grid_cells, dtype=jnp.int32), grid_cells)[None, :]
    wave_cols = wave_numbers(col_index, grid_cells)[:, None]
    square_sum = jnp.maximum(wave_rows * wave_rows + wave_cols * wave_cols, 1.0)
    first_factor = (wave_rows * wave_rows - wave_cols * wave_cols) / square_sum
    second_factor = 2.0 * wave_rows * wave_cols / square_sum
    kernel_real = first_factor * freq_real - second_factor * freq_imag
    kernel_imag = first_factor * freq_imag + second_factor * freq_real
    back_real, back_imag = fourier(kernel_real, kernel_imag, True)
    returned = jnp.stack([back_real, back_imag]).transpose(0, 3, 1, 2)
    rows_local = lax.all_to_all(
        lax.all_to_all(returned, "trans", split_axis=1, concat_axis=3, tiled=True),
        "los",
        split_axis=1,
        concat_axis=3,
        tiled=True,
    )
    final_real, final_imag = fourier(rows_local[0], rows_local[1], True)
    return jnp.stack([final_real, final_imag]).transpose(0, 2, 1, 3)


def solution(mesh):
    placed = (P("los", "trans", None), P(), P(), P(), P(), P())
    return jax.shard_map(
        body,
        mesh=mesh,
        in_specs=placed,
        out_specs=P(None, None, ("trans", "los"), None),
        check_vma=False,
    )
```

profile of v0, /device:TPU:0, one launch (start us, length us, event | category | flops | bytes accessed | tf_op | source)
XLA Modules:
  0.0 628.0 jit_solution(389081637381458077)
XLA Ops:
  9.4 11.4 %reduce = bf16[2048,128]{1,0:T(8,128)(2,1)S(1)} reduce(bf16[2048,1,128]{2,1,0:T(2,128)(2,1)S(1)} %bitcast.333, bf16[]{:T(256)} %broadcast.788), dimensions={1}, to_apply=%bitcast.274.reduce_sub_computation | reduce | bytes 1048578
  21.8 8.9 %all-to-all-start = ((bf16[16,2,8192]{2,1,0:T(2,128)(2,1)}), bf16[16,2,8192]{2,1,0:T(2,128)(2,1)S(1)}, u32[]{:S(2)}, u32[]{:S(2)}) async-start(bf16[16,2,8192]{2,1,0:T(2,128)(2,1)} %reshape.416), calls=%async_computation | async-start | bytes 1048576 | tf_op jit(solution)/shard_map/all_to_all | solution.py:73
  32.2 13.6 %all-to-all-done = bf16[16,2,8192]{2,1,0:T(2,128)(2,1)S(1)} async-done(((bf16[16,2,8192]{2,1,0:T(2,128)(2,1)}), bf16[16,2,8192]{2,1,0:T(2,128)(2,1)S(1)}, u32[]{:S(2)}, u32[]{:S(2)}) %all-to-all-start) | async-done | bytes 524320 | tf_op jit(solution)/shard_map/all_to_all | solution.py:73
  61.7 8.1 %copy.182 = bf16[1,128,2048]{1,0,2:T(2,128)(2,1)S(1)} copy(bf16[1,128,2048]{1,2,0:T(8,128)(2,1)S(1)} %pad_maximum_fusion.1) | data formatting | bytes 1048576 | tf_op jit(solution)/shard_map/concatenate | solution.py:94
  69.9 11.6 %reduce.1 = bf16[2048,128]{1,0:T(8,128)(2,1)S(1)} reduce(bf16[2048,1,128]{2,1,0:T(2,128)(2,1)S(1)} %bitcast.334, bf16[]{:T(256)} %broadcast.788), dimensions={1}, to_apply=%bitcast.300.reduce_sub_computation | reduce | bytes 1048578
  88.5 12.4 %all-to-all-done.1 = bf16[16,2,8192]{2,1,0:T(2,128)(2,1)S(1)} async-done(((bf16[16,2,8192]{2,1,0:T(2,128)(2,1)}), bf16[16,2,8192]{2,1,0:T(2,128)(2,1)S(1)}, u32[]{:S(2)}, u32[]{:S(2)}) %all-to-all-start.1) | async-done | bytes 524320 | tf_op jit(solution)/shard_map/all_to_all | solution.py:97
  102.0 12.7 %fusion.8 = f32[128,16,128]{2,0,1:T(8,128)S(1)} fusion(bf16[2048,128,1]{0,1,2:T(8,128)(2,1)S(1)} %reshape.400, f32[2048]{0:T(1024)S(1)} %iota_convert_fusion, f32[16,128]{1,0:T(8,128)S(1)} %bitcast.343), kind=kOutput, calls=%fused_computation.12 | convolution fusion | flops 1128267776 | bytes 1589248 | tf_op jit(solution)/shard_map/dot_general | solution.py:99
  128.5 6.5 %fusion.52 = f32[128,4,16,128]{0,3,2,1:T(8,128)S(1)} fusion(f32[128,4,16,128]{3,2,1,0:T(8,128)S(1)} %get-tuple-element.10), kind=kOutput, calls=%fused_computation.75 | convolution fusion | flops 1610858496 | bytes 8388608 | tf_op jit(solution)/shard_map/...km,mj->...kj/dot_general | solution.py:47
  135.1 6.7 %subtract_bitcast_fusion = f32[128,4,128,16]{0,2,3,1:T(8,128)S(1)} fusion(f32[128,4,16,128]{0,3,2,1:T(8,128)S(1)} %fusion.52, f32[128,4,16,128]{3,2,1,0:T(8,128)S(1)} %get-tuple-element.9), kind=kOutput, calls=%fused_computation.56 | convolution fusion | flops 1611890688 | bytes 12582912 | tf_op jit(solution)/shard_map/...km,mj->...kj/dot_general | solution.py:47
  146.2 9.4 %fusion.50 = f32[128,4,16,128]{0,3,2,1:T(8,128)S(1)} fusion(f32[128,4,16,128]{3,2,1,0:T(8,128)} %copy-done.5), kind=kOutput, calls=%fused_computation.73 | convolution fusion | flops 1610842112 | bytes 8388608 | tf_op jit(solution)/shard_map/...km,mj->...kj/dot_general | solution.py:47
  155.7 6.5 %add_bitcast_fusion = f32[128,4,128,16]{0,2,3,1:T(8,128)S(1)} fusion(f32[128,4,16,128]{0,3,2,1:T(8,128)S(1)} %fusion.50, f32[128,4,16,128]{3,2,1,0:T(8,128)S(1)} %copy-done.4), kind=kOutput, calls=%fused_computation.55 | convolution fusion | flops 1611907072 | bytes 12582912 | tf_op jit(solution)/shard_map/...km,mj->...kj/dot_general | solution.py:47
  166.7 10.4 %reduce-scatter.5.cloned.1.call-done = f32[128,4,1024]{0,2,1:T(8,128)} async-done(((f32[128,4,2048]{0,2,1:T(8,128)}), f32[128,4,1024]{0,2,1:T(8,128)}) %reduce-scatter.5.cloned.1.call-update) | async-done | bytes 2097168 | tf_op jit(solution)/shard_map/reduce_scatter | solution.py:109
  184.6 7.0 %all-to-all-start.2 = ((f32[2,128,4,1024]{1,2,0,3:T(4,128)}), f32[2,128,4,1024]{1,2,0,3:T(4,128)}, u32[]{:S(2)}, u32[]{:S(2)}) async-start(f32[2,128,4,1024]{1,2,0,3:T(4,128)} %copy.123), calls=%async_computation.4 | async-start | bytes 8388608 | tf_op jit(solution)/shard_map/all_to_all | solution.py:111
  193.2 78.7 %all-to-all-done.2 = f32[2,128,4,1024]{1,2,0,3:T(4,128)} async-done(((f32[2,128,4,1024]{1,2,0,3:T(4,128)}), f32[2,128,4,1024]{1,2,0,3:T(4,128)}, u32[]{:S(2)}, u32[]{:S(2)}) %all-to-all-start.2) | async-done | bytes 4194336 | tf_op jit(solution)/shard_map/all_to_all | solution.py:111
  308.6 8.7 %fusion.34 = (f32[4,64,16,128]{1,3,2,0:T(8,128)}, f32[4,64,16,128]{1,3,2,0:T(8,128)}) fusion(f32[64,16,128]{0,2,1:T(8,128)S(1)} %copy-done.15, f32[64,16,128]{0,2,1:T(8,128)S(1)} %get-tuple-element.15, f32[4,64,16,128]{1,3,2,0:T(8,128)} %bitcast.325, f32[4,64,16,128]{1,3,2,0:T(8,128)} %bitcast.323), kind=kLoop, calls=%fused_computation.45 | loop fusion | flops 3145728 | bytes 9437184 | tf_op jit(solution)/shard_map/sub | solution.py:126
  364.1 15.3 %copy.181 = f32[2,2048,4,64]{3,2,0,1:T(4,128)} copy(f32[2,2048,4,64]{3,1,2,0:T(8,128)S(1)} %maximum_bitcast_fusion) | data formatting | bytes 8388608 | tf_op jit(solution)/shard_map/transpose | solution.py:129
  379.4 14.6 %reshape.420 = f32[16,1,65536]{2,1,0:T(1,128)} reshape(f32[2048,2,4,64]{3,2,1,0:T(4,128)} %bitcast.312) | data formatting | bytes 8388608
  393.9 113.6 %all_to_all.81 = f32[16,1,65536]{2,1,0:T(1,128)} all-to-all(f32[16,1,65536]{2,1,0:T(1,128)} %reshape.420), channel_id=1, replica_groups=mesh['trans'=16,'los'=2] {'trans'}, dimensions={0} | all-to-all | bytes 8388608 | tf_op jit(solution)/shard_map/all_to_all | solution.py:131
  508.2 13.8 %reduce.2 = f32[16,65536]{1,0:T(8,128)} reduce(f32[16,1,65536]{2,1,0:T(1,128)} %all_to_all.81, f32[]{:T(128)} %broadcast.790), dimensions={1}, to_apply=%all_to_all.69.reduce_sub_computation | reduce | bytes 8388612 | tf_op jit(solution)/shard_map/all_to_all | solution.py:131
  522.0 9.3 %reshape.421 = f32[2048,2,4,64]{3,2,1,0:T(4,128)} reshape(f32[16,65536]{1,0:T(8,128)} %reduce.2) | data formatting | bytes 8388608
  531.2 8.5 %copy.159 = f32[2,16,128,4,64]{2,4,1,3,0:T(8,128)} copy(f32[2,16,128,4,64]{4,3,0,2,1:T(4,128)} %bitcast.311) | data formatting | bytes 8388608 | tf_op jit(solution)/shard_map/all_to_all | solution.py:131
  545.3 8.6 %all_to_all.82 = f32[2,128,4,1024]{3,2,0,1:T(4,128)S(1)} all-to-all(f32[2,128,4,1024]{3,2,0,1:T(4,128)} %copy.137), channel_id=1, replica_groups=mesh['trans'=16,'los'=2] {'los'}, dimensions={1} | all-to-all | bytes 8388608 | tf_op jit(solution)/shard_map/all_to_all | solution.py:130
  606.9 7.2 %maximum_bitcast_fusion.1 = f32[2,4,64,2048]{2,3,1,0:T(8,128)} fusion(f32[1,64,4,2048]{1,3,2,0:T(8,128)} %bitcast.328, f32[1,64,4,2048]{1,3,2,0:T(8,128)} %bitcast.324), kind=kLoop, calls=%fused_computation.11 | loop fusion | flops 1048576 | bytes 8388608 | tf_op jit(solution)/shard_map/transpose | solution.py:138
  614.1 6.8 %copy.143 = f32[2,4,64,2048]{3,2,1,0:T(8,128)} copy(f32[2,4,64,2048]{2,3,1,0:T(8,128)} %maximum_bitcast_fusion.1) | data formatting | bytes 8388608 | tf_op jit(solution)/shard_map/transpose | solution.py:138
  (133 shorter events, 203.1 us)
Async XLA Ops:
  8.9 21.8 %copy-start.19 = (s32[2]{0:T(128)S(1)}, s32[2]{0:T(128)}, u32[]{:S(2)}) copy-start(s32[2]{0:T(128)} %param.9) | copy-start | bytes 28
  8.9 23.1 %copy-start.16 = (f32[2,2048]{1,0:T(2,128)S(1)}, f32[2,2048]{1,0:T(2,128)}, u32[]{:S(2)}) copy-start(f32[2,2048]{1,0:T(2,128)} %param.8) | copy-start | bytes 49156
  8.9 23.1 %copy-start.17 = (f32[2,2048]{1,0:T(2,128)S(1)}, f32[2,2048]{1,0:T(2,128)}, u32[]{:S(2)}) copy-start(f32[2,2048]{1,0:T(2,128)} %param.7) | copy-start | bytes 49156
  21.8 23.9 %all-to-all-start = ((bf16[16,2,8192]{2,1,0:T(2,128)(2,1)}), bf16[16,2,8192]{2,1,0:T(2,128)(2,1)S(1)}, u32[]{:S(2)}, u32[]{:S(2)}) async-start(bf16[16,2,8192]{2,1,0:T(2,128)(2,1)} %reshape.416), calls=%async_computation | async-start | bytes 1048576 | tf_op jit(solution)/shard_map/all_to_all | solution.py:73
  69.9 16.6 %copy-start.20 = (s32[2]{0:T(128)S(1)}, s32[2]{0:T(128)}, u32[]{:S(2)}) copy-start(s32[2]{0:T(128)} %param.10) | copy-start | bytes 28
  69.9 17.9 %copy-start.18 = (f32[4,2]{0,1:T(2,128)S(1)}, f32[4,2]{0,1:T(2,128)}, u32[]{:S(2)}) copy-start(f32[4,2]{0,1:T(2,128)} %param.11) | copy-start | bytes 100
  82.4 18.4 %all-to-all-start.1 = ((bf16[16,2,8192]{2,1,0:T(2,128)(2,1)}), bf16[16,2,8192]{2,1,0:T(2,128)(2,1)S(1)}, u32[]{:S(2)}, u32[]{:S(2)}) async-start(bf16[16,2,8192]{2,1,0:T(2,128)(2,1)} %reshape.418), calls=%async_computation.1 | async-start | bytes 1048576 | tf_op jit(solution)/shard_map/all_to_all | solution.py:97
  86.4 80.3 %reduce-scatter.3.cloned.1.call-start = ((), (), s32[]{:S(2)}) async-start(), calls=%async_computation.7 | async-start | bytes 6291456 | tf_op jit(solution)/shard_map/reduce_scatter | solution.py:108
  128.5 6.5 %copy-start.5 = (f32[128,4,16,128]{3,2,1,0:T(8,128)}, f32[128,4,16,128]{3,2,1,0:T(8,128)S(1)}, u32[]{:S(2)}) copy-start(f32[128,4,16,128]{3,2,1,0:T(8,128)S(1)} %get-tuple-element.10) | copy-start | bytes 12582916
  128.5 6.5 %copy-start.3 = (f32[128,4,16,128]{3,2,1,0:T(8,128)}, f32[128,4,16,128]{3,2,1,0:T(8,128)S(1)}, u32[]{:S(2)}) copy-start(f32[128,4,16,128]{3,2,1,0:T(8,128)S(1)} %get-tuple-element.9) | copy-start | bytes 12582916
  146.2 31.0 %reduce-scatter.5.cloned.1.call-start = ((), (), s32[]{:S(2)}) async-start(), calls=%async_computation.8 | async-start | bytes 6291456 | tf_op jit(solution)/shard_map/reduce_scatter | solution.py:109
  146.2 9.5 %copy-start.4 = (f32[128,4,16,128]{3,2,1,0:T(8,128)S(1)}, f32[128,4,16,128]{3,2,1,0:T(8,128)}, u32[]{:S(2)}) copy-start(f32[128,4,16,128]{3,2,1,0:T(8,128)} %copy-done.3) | copy-start | bytes 12582916
  184.6 87.3 %all-to-all-start.2 = ((f32[2,128,4,1024]{1,2,0,3:T(4,128)}), f32[2,128,4,1024]{1,2,0,3:T(4,128)}, u32[]{:S(2)}, u32[]{:S(2)}) async-start(f32[2,128,4,1024]{1,2,0,3:T(4,128)} %copy.123), calls=%async_computation.4 | async-start | bytes 8388608 | tf_op jit(solution)/shard_map/all_to_all | solution.py:111
  284.6 6.0 copy-start.1
  304.1 4.5 copy-start.15
  320.4 3.3 copy-start.6
  328.3 2.0 copy-start.13
  330.2 3.7 copy-start.7
  336.0 5.6 copy-start.2
  564.0 3.3 copy-start.9
  564.0 3.3 copy-start.14
  574.7 2.0 copy-start.12
  576.7 3.7 copy-start.10
  582.4 5.6 copy-start
  (2 other events, 2.6 us)
Sparse Core Ops, SparseCore 0:
  146.3 10.2 reduce-scatter.2
  166.8 10.2 reduce-scatter.4
where the time goes:
time: 634 us; the launch traced here: 628 us
  local copies, waits for them, and re-layouts  147 us (23%)
  matrix products  145 us (23%)
  blocking collectives  122 us (19%)
  waiting for transfers between devices  115 us (18%)
  other arithmetic  64.5 us (10%)
  starting transfers between devices  19.9 us (3%)
  between operations  14.4 us (2%)
    all_to_all x1, blocking collectives, body(): lax.all_to_all(returned, 'trans', split_axis=1, concat_axis=3, tiled=True)  114 us
    all_to_all x1, waiting for transfers between devices, body(): lax.all_to_all(jnp.stack([summed_real, summed_imag]), 'trans', split_axis...  78.7 us
    dot_general x16, matrix products, second_pass(): return jnp.einsum('...km,mj->...kj', values, table, precision=highest)  74.2 us
    dot_general x16, matrix products, first_pass(): return jnp.einsum('kn,...nm->...km', table, values, precision=highest)  42.8 us
    unnamed x54, local copies, waits for them, and re-layouts  33.2 us
    unnamed x2, other arithmetic  23.1 us
    mul x4, local copies, waits for them, and re-layouts, fourier(): return (out_real * scale, out_imag * scale)  18.3 us
    transpose x1, local copies, waits for them, and re-layouts, body(): returned = jnp.stack([back_real, back_imag]).transpose(0, 3, 1, 2)  15.3 us
  transfers between devices with their start and end apart: 5, of which 4 were waited for; matrix products, arithmetic and copies ran while one was open for 4% of the time, Pallas kernels for 0%

commit v1 on v0

--- a/solution.py
+++ b/solution.py
@@ -128,7 +128,12 @@
     back_real, back_imag = fourier(kernel_real, kernel_imag, True)
     returned = jnp.stack([back_real, back_imag]).transpose(0, 3, 1, 2)
     rows_local = lax.all_to_all(
-        lax.all_to_all(returned, "trans", split_axis=1, concat_axis=3, tiled=True),
+        jnp.concatenate(
+            lax.all_to_all(
+                jnp.stack(jnp.split(returned, lax.axis_size("trans"), axis=1)), "trans", 0, 0
+            ),
+            axis=3,
+        ),
         "los",
         split_axis=1,
         concat_axis=3,

time: 634 us -> 594 us (0.937)
  local copies, waits for them, and re-layouts: 147 us -> 121 us
  other arithmetic: 64.5 us -> 51 us
    transpose x1 -> x0, local copies, waits for them, and re-layouts: 15.3 us -> none  [body(): returned = jnp.stack([back_real, back_imag]).transpose(0, 3, 1, 2)]
    unnamed x54 -> x63, local copies, waits for them, and re-layouts: 33.2 us -> 19.3 us
    all_to_all x1 -> x0, other arithmetic: 13.8 us -> none  [body(): lax.all_to_all(returned, 'trans', split_axis=1, concat_axis=3, tiled=True)]
    all_to_all x4 -> x2, local copies, waits for them, and re-layouts: 17.1 us -> 4.75 us  [the longest x1 2.43 us: body(): lax.all_to_all(jnp.concatenate(lax.all_to_all(jnp.stack(jnp.split(returne...]
    another operation x0 -> x2, local copies, waits for them, and re-layouts: none -> 7.63 us  [body(): jnp.stack(jnp.split(returned, lax.axis_size('trans'), axis=1))]
where the time goes in v1:
time: 594 us; the launch traced here: 588 us
  matrix products  145 us (24%)
  blocking collectives  122 us (21%)
  local copies, waits for them, and re-layouts  121 us (20%)
  waiting for transfers between devices  115 us (19%)
  other arithmetic  51 us (9%)
  starting transfers between devices  19.5 us (3%)
  between operations  14.4 us (2%)
    all_to_all x1, blocking collectives, body(): lax.all_to_all(jnp.stack(jnp.split(returned, lax.axis_size('trans'), axis...  114 us
    all_to_all x1, waiting for transfers between devices, body(): lax.all_to_all(jnp.stack([summed_real, summed_imag]), 'trans', split_axis...  78.7 us
    dot_general x16, matrix products, second_pass(): return jnp.einsum('...km,mj->...kj', values, table, precision=highest)  74 us
    dot_general x16, matrix products, first_pass(): return jnp.einsum('kn,...nm->...km', table, values, precision=highest)  43.1 us
    unnamed x2, other arithmetic  23.4 us
    unnamed x63, local copies, waits for them, and re-layouts  19.3 us
    mul x4, local copies, waits for them, and re-layouts, fourier(): return (out_real * scale, out_imag * scale)  18.4 us
    dot_general x4, matrix products, body(): lax.dot_general(by_columns[local_slot], row_block, (((0,), (1,)), ((), ()...  15 us
  transfers between devices with their start and end apart: 5, of which 4 were waited for; matrix products, arithmetic and copies ran while one was open for 4% of the time, Pallas kernels for 0%

profile of v1, /device:TPU:0, one launch (start us, length us, event | category | flops | bytes accessed | tf_op | source)
XLA Modules:
  0.0 588.3 jit_solution(5901417749141465328)
XLA Ops:
  9.5 11.5 %reduce = bf16[2048,128]{1,0:T(8,128)(2,1)S(1)} reduce(bf16[2048,1,128]{2,1,0:T(2,128)(2,1)S(1)} %bitcast.389, bf16[]{:T(256)} %broadcast.788), dimensions={1}, to_apply=%bitcast.336.reduce_sub_computation | reduce | bytes 1048578
  21.9 8.5 %all-to-all-start = ((bf16[16,2,8192]{2,1,0:T(2,128)(2,1)}), bf16[16,2,8192]{2,1,0:T(2,128)(2,1)S(1)}, u32[]{:S(2)}, u32[]{:S(2)}) async-start(bf16[16,2,8192]{2,1,0:T(2,128)(2,1)} %reshape.424), calls=%async_computation | async-start | bytes 1048576 | tf_op jit(solution)/shard_map/all_to_all | solution.py:73
  31.8 13.7 %all-to-all-done = bf16[16,2,8192]{2,1,0:T(2,128)(2,1)S(1)} async-done(((bf16[16,2,8192]{2,1,0:T(2,128)(2,1)}), bf16[16,2,8192]{2,1,0:T(2,128)(2,1)S(1)}, u32[]{:S(2)}, u32[]{:S(2)}) %all-to-all-start) | async-done | bytes 524320 | tf_op jit(solution)/shard_map/all_to_all | solution.py:73
  61.5 8.1 %copy.178 = bf16[1,128,2048]{1,0,2:T(2,128)(2,1)S(1)} copy(bf16[1,128,2048]{1,2,0:T(8,128)(2,1)S(1)} %pad_maximum_fusion.1) | data formatting | bytes 1048576 | tf_op jit(solution)/shard_map/concatenate | solution.py:94
  69.6 11.9 %reduce.1 = bf16[2048,128]{1,0:T(8,128)(2,1)S(1)} reduce(bf16[2048,1,128]{2,1,0:T(2,128)(2,1)S(1)} %bitcast.390, bf16[]{:T(256)} %broadcast.788), dimensions={1}, to_apply=%bitcast.358.reduce_sub_computation | reduce | bytes 1048578
  88.5 12.3 %all-to-all-done.1 = bf16[16,2,8192]{2,1,0:T(2,128)(2,1)S(1)} async-done(((bf16[16,2,8192]{2,1,0:T(2,128)(2,1)}), bf16[16,2,8192]{2,1,0:T(2,128)(2,1)S(1)}, u32[]{:S(2)}, u32[]{:S(2)}) %all-to-all-start.1) | async-done | bytes 524320 | tf_op jit(solution)/shard_map/all_to_all | solution.py:97
  102.0 12.5 %fusion.8 = f32[128,16,128]{2,0,1:T(8,128)S(1)} fusion(bf16[2048,128,1]{0,1,2:T(8,128)(2,1)S(1)} %reshape.408, f32[2048]{0:T(1024)S(1)} %iota_convert_fusion, f32[16,128]{1,0:T(8,128)S(1)} %bitcast.399), kind=kOutput, calls=%fused_computation.12 | convolution fusion | flops 1128267776 | bytes 1589248 | tf_op jit(solution)/shard_map/dot_general | solution.py:99
  128.4 6.5 %fusion.52 = f32[128,4,16,128]{0,3,2,1:T(8,128)S(1)} fusion(f32[128,4,16,128]{3,2,1,0:T(8,128)S(1)} %get-tuple-element.10), kind=kOutput, calls=%fused_computation.75 | convolution fusion | flops 1610858496 | bytes 8388608 | tf_op jit(solution)/shard_map/...km,mj->...kj/dot_general | solution.py:47
  134.9 6.9 %subtract_bitcast_fusion = f32[128,4,128,16]{0,2,3,1:T(8,128)S(1)} fusion(f32[128,4,16,128]{0,3,2,1:T(8,128)S(1)} %fusion.52, f32[128,4,16,128]{3,2,1,0:T(8,128)S(1)} %get-tuple-element.9), kind=kOutput, calls=%fused_computation.56 | convolution fusion | flops 1611890688 | bytes 12582912 | tf_op jit(solution)/shard_map/...km,mj->...kj/dot_general | solution.py:47
  146.3 9.2 %fusion.50 = f32[128,4,16,128]{0,3,2,1:T(8,128)S(1)} fusion(f32[128,4,16,128]{3,2,1,0:T(8,128)} %copy-done.5), kind=kOutput, calls=%fused_computation.73 | convolution fusion | flops 1610842112 | bytes 8388608 | tf_op jit(solution)/shard_map/...km,mj->...kj/dot_general | solution.py:47
  155.5 6.5 %add_bitcast_fusion = f32[128,4,128,16]{0,2,3,1:T(8,128)S(1)} fusion(f32[128,4,16,128]{0,3,2,1:T(8,128)S(1)} %fusion.50, f32[128,4,16,128]{3,2,1,0:T(8,128)S(1)} %copy-done.4), kind=kOutput, calls=%fused_computation.55 | convolution fusion | flops 1611907072 | bytes 12582912 | tf_op jit(solution)/shard_map/...km,mj->...kj/dot_general | solution.py:47
  166.5 10.4 %reduce-scatter.5.cloned.1.call-done = f32[128,4,1024]{0,2,1:T(8,128)} async-done(((f32[128,4,2048]{0,2,1:T(8,128)}), f32[128,4,1024]{0,2,1:T(8,128)}) %reduce-scatter.5.cloned.1.call-update) | async-done | bytes 2097168 | tf_op jit(solution)/shard_map/reduce_scatter | solution.py:109
  184.6 7.0 %all-to-all-start.2 = ((f32[2,128,4,1024]{1,2,0,3:T(4,128)}), f32[2,128,4,1024]{1,2,0,3:T(4,128)}, u32[]{:S(2)}, u32[]{:S(2)}) async-start(f32[2,128,4,1024]{1,2,0,3:T(4,128)} %copy.124), calls=%async_computation.4 | async-start | bytes 8388608 | tf_op jit(solution)/shard_map/all_to_all | solution.py:111
  193.2 78.7 %all-to-all-done.2 = f32[2,128,4,1024]{1,2,0,3:T(4,128)} async-done(((f32[2,128,4,1024]{1,2,0,3:T(4,128)}), f32[2,128,4,1024]{1,2,0,3:T(4,128)}, u32[]{:S(2)}, u32[]{:S(2)}) %all-to-all-start.2) | async-done | bytes 4194336 | tf_op jit(solution)/shard_map/all_to_all | solution.py:111
  298.3 5.6 subtract_bitcast_fusion.1
  308.4 8.8 %fusion.34 = (f32[4,64,16,128]{1,3,2,0:T(8,128)}, f32[4,64,16,128]{1,3,2,0:T(8,128)}) fusion(f32[64,16,128]{0,2,1:T(8,128)S(1)} %copy-done.13, f32[64,16,128]{0,2,1:T(8,128)S(1)} %get-tuple-element.15, f32[4,64,16,128]{1,3,2,0:T(8,128)} %bitcast.379, f32[4,64,16,128]{1,3,2,0:T(8,128)} %bitcast.381), kind=kLoop, calls=%fused_computation.45 | loop fusion | flops 3145728 | bytes 9437184 | tf_op jit(solution)/shard_map/sub | solution.py:126
  350.2 5.6 multiply_bitcast_fusion.3
  377.8 6.8 %copy.135 = f32[16,2,128,4,64]{2,4,3,1,0:T(8,128)} copy(f32[16,2,128,4,64]{4,2,3,1,0:T(8,128)} %fusion.139) | data formatting | bytes 8388608 | tf_op jit(solution)/shard_map/stack | solution.py:133
  384.5 113.5 %all_to_all.68 = f32[16,2,128,4,64]{2,4,3,1,0:T(8,128)S(1)} all-to-all(f32[16,2,128,4,64]{2,4,3,1,0:T(8,128)} %copy.135), channel_id=1, replica_groups=mesh['trans'=16,'los'=2] {'trans'}, dimensions={0} | all-to-all | bytes 8388608 | tf_op jit(solution)/shard_map/all_to_all | solution.py:132
  500.4 5.5 copy.137
  505.9 8.6 %all_to_all.69 = f32[2,128,4,1024]{3,2,0,1:T(4,128)S(1)} all-to-all(f32[2,128,4,1024]{3,2,0,1:T(4,128)} %copy.137), channel_id=1, replica_groups=mesh['trans'=16,'los'=2] {'los'}, dimensions={1} | all-to-all | bytes 8388608 | tf_op jit(solution)/shard_map/all_to_all | solution.py:130
  556.8 5.6 multiply_bitcast_fusion.1
  567.2 7.2 %maximum_bitcast_fusion.1 = f32[2,4,64,2048]{2,3,1,0:T(8,128)} fusion(f32[1,64,4,2048]{1,3,2,0:T(8,128)} %bitcast.380, f32[1,64,4,2048]{1,3,2,0:T(8,128)} %bitcast.384), kind=kLoop, calls=%fused_computation.11 | loop fusion | flops 1048576 | bytes 8388608 | tf_op jit(solution)/shard_map/transpose | solution.py:143
  574.4 6.8 %copy.143 = f32[2,4,64,2048]{3,2,1,0:T(8,128)} copy(f32[2,4,64,2048]{2,3,1,0:T(8,128)} %maximum_bitcast_fusion.1) | data formatting | bytes 8388608 | tf_op jit(solution)/shard_map/transpose | solution.py:143
  (141 shorter events, 196.0 us)
Async XLA Ops:
  6.5 23.9 %copy-start.17 = (s32[2]{0:T(128)S(1)}, s32[2]{0:T(128)}, u32[]{:S(2)}) copy-start(s32[2]{0:T(128)} %param.9) | copy-start | bytes 28
  6.5 25.1 %copy-start.14 = (f32[2,2048]{1,0:T(2,128)S(1)}, f32[2,2048]{1,0:T(2,128)}, u32[]{:S(2)}) copy-start(f32[2,2048]{1,0:T(2,128)} %param.8) | copy-start | bytes 49156
  6.5 25.1 %copy-start.15 = (f32[2,2048]{1,0:T(2,128)S(1)}, f32[2,2048]{1,0:T(2,128)}, u32[]{:S(2)}) copy-start(f32[2,2048]{1,0:T(2,128)} %param.7) | copy-start | bytes 49156
  21.9 23.6 %all-to-all-start = ((bf16[16,2,8192]{2,1,0:T(2,128)(2,1)}), bf16[16,2,8192]{2,1,0:T(2,128)(2,1)S(1)}, u32[]{:S(2)}, u32[]{:S(2)}) async-start(bf16[16,2,8192]{2,1,0:T(2,128)(2,1)} %reshape.424), calls=%async_computation | async-start | bytes 1048576 | tf_op jit(solution)/shard_map/all_to_all | solution.py:73
  61.4 25.1 %copy-start.18 = (s32[2]{0:T(128)S(1)}, s32[2]{0:T(128)}, u32[]{:S(2)}) copy-start(s32[2]{0:T(128)} %param.10) | copy-start | bytes 28
  61.4 26.3 %copy-start.16 = (f32[4,2]{0,1:T(2,128)S(1)}, f32[4,2]{0,1:T(2,128)}, u32[]{:S(2)}) copy-start(f32[4,2]{0,1:T(2,128)} %param.11) | copy-start | bytes 100
  82.5 18.4 %all-to-all-start.1 = ((bf16[16,2,8192]{2,1,0:T(2,128)(2,1)}), bf16[16,2,8192]{2,1,0:T(2,128)(2,1)S(1)}, u32[]{:S(2)}, u32[]{:S(2)}) async-start(bf16[16,2,8192]{2,1,0:T(2,128)(2,1)} %reshape.426), calls=%async_computation.1 | async-start | bytes 1048576 | tf_op jit(solution)/shard_map/all_to_all | solution.py:97
  86.4 80.1 %reduce-scatter.3.cloned.1.call-start = ((), (), s32[]{:S(2)}) async-start(), calls=%async_computation.7 | async-start | bytes 6291456 | tf_op jit(solution)/shard_map/reduce_scatter | solution.py:108
  128.4 6.5 %copy-start.5 = (f32[128,4,16,128]{3,2,1,0:T(8,128)}, f32[128,4,16,128]{3,2,1,0:T(8,128)S(1)}, u32[]{:S(2)}) copy-start(f32[128,4,16,128]{3,2,1,0:T(8,128)S(1)} %get-tuple-element.10) | copy-start | bytes 12582916
  128.4 6.5 %copy-start.3 = (f32[128,4,16,128]{3,2,1,0:T(8,128)}, f32[128,4,16,128]{3,2,1,0:T(8,128)S(1)}, u32[]{:S(2)}) copy-start(f32[128,4,16,128]{3,2,1,0:T(8,128)S(1)} %get-tuple-element.9) | copy-start | bytes 12582916
  146.2 30.7 %reduce-scatter.5.cloned.1.call-start = ((), (), s32[]{:S(2)}) async-start(), calls=%async_computation.8 | async-start | bytes 6291456 | tf_op jit(solution)/shard_map/reduce_scatter | solution.py:109
  146.3 9.2 %copy-start.4 = (f32[128,4,16,128]{3,2,1,0:T(8,128)S(1)}, f32[128,4,16,128]{3,2,1,0:T(8,128)}, u32[]{:S(2)}) copy-start(f32[128,4,16,128]{3,2,1,0:T(8,128)} %copy-done.3) | copy-start | bytes 12582916
  184.6 87.3 %all-to-all-start.2 = ((f32[2,128,4,1024]{1,2,0,3:T(4,128)}), f32[2,128,4,1024]{1,2,0,3:T(4,128)}, u32[]{:S(2)}, u32[]{:S(2)}) async-start(f32[2,128,4,1024]{1,2,0,3:T(4,128)} %copy.124), calls=%async_computation.4 | async-start | bytes 8388608 | tf_op jit(solution)/shard_map/all_to_all | solution.py:111
  284.6 5.8 copy-start.1
  303.9 4.5 copy-start.13
  320.2 8.3 %copy-start.6 = (f32[4,64,16,128]{3,2,1,0:T(8,128)}, f32[4,64,16,128]{3,2,1,0:T(8,128)S(1)}, u32[]{:S(2)}) copy-start(f32[4,64,16,128]{3,2,1,0:T(8,128)S(1)} %copy.129) | copy-start | bytes 6291460
  330.5 3.7 copy-start.7
  336.3 6.0 %copy-start.2 = (f32[4,64,128,16]{2,3,1,0:T(8,128)}, f32[4,64,128,16]{2,3,1,0:T(8,128)S(1)}, u32[]{:S(2)}) copy-start(f32[4,64,128,16]{2,3,1,0:T(8,128)S(1)} %convolution_subtract_fusion.2) | copy-start | bytes 6291460
  524.6 6.2 %copy-start.8 = (f32[64,4,16,128]{3,2,1,0:T(8,128)}, f32[64,4,16,128]{3,2,1,0:T(8,128)S(1)}, u32[]{:S(2)}) copy-start(f32[64,4,16,128]{3,2,1,0:T(8,128)S(1)} %reshape_squeeze.14) | copy-start | bytes 6291460
  524.6 3.3 copy-start.12
  534.9 3.7 copy-start.10
  534.9 3.7 copy-start.11
  538.7 2.0 copy-start.9
  542.7 5.6 copy-start
Sparse Core Ops, SparseCore 0:
  146.3 10.2 reduce-scatter.2
  166.6 10.2 reduce-scatter.4
